TPU v7x, 32 devices: a whole 2x2x4 slice. The times are simulated.
32 devices in a mesh: seq: 4 (over y, x), fsdp: 8 (over z, core).
Axes of the slice: x: 2, y: 2, z: 4, core: 2. Of those that a mesh axis runs over, the one named last changes fastest.
Arguments:
- images: bfloat16 [24, 512, 1152], P('fsdp', 'seq'), may hold values from -6 to 6
- key_mask: int32 [24, 512], P('fsdp'), may hold values from 0 to 1, as said below
- attn_gain: bfloat16 [1152], P('fsdp'), may hold values from 0.25 to 1.75
- attn_shift: bfloat16 [1152], P('fsdp'), may hold values from -3 to 3
- query_weight: bfloat16 [1152, 1152], P('fsdp'), may hold values from -0.1875 to 0.1875
- key_weight: bfloat16 [1152, 1152], P('fsdp'), may hold values from -0.1875 to 0.1875
- value_weight: bfloat16 [1152, 1152], P('fsdp'), may hold values from -0.1875 to 0.1875
- query_bias: bfloat16 [1152], P('fsdp'), may hold values from -3 to 3
- value_bias: bfloat16 [1152], P('fsdp'), may hold values from -0.1796875 to 0.1796875
- out_weight: bfloat16 [1152, 1152], P('fsdp'), may hold values from -1.5 to 1.5
- out_bias: bfloat16 [1152], P('fsdp'), may hold values from -3 to 3
- mlp_gain: bfloat16 [1152], P('fsdp'), may hold values from 0.25 to 1.75
- mlp_shift: bfloat16 [1152], P('fsdp'), may hold values from -3 to 3
- inner_weight: bfloat16 [1152, 4304], P('fsdp'), may hold values from -0.1875 to 0.1875
- inner_bias: bfloat16 [4304], P('fsdp'), may hold values from -3 to 3
- outer_weight: bfloat16 [4304, 1152], P('fsdp'), may hold values from -0.09375 to 0.09375
- outer_bias: bfloat16 [1152], P('fsdp'), may hold values from -3 to 3
- cotangent: bfloat16 [24, 512, 1152], P('fsdp', 'seq'), may hold values from -6 to 6
Outputs:
- layer_out: float32 [24, 512, 1152], P('fsdp', 'seq')
- images_grad: float32 [24, 512, 1152], P('fsdp', 'seq')
- attn_gain_grad: float32 [1152], P('fsdp')
- attn_shift_grad: float32 [1152], P('fsdp')
- query_weight_grad: float32 [1152, 1152], P('fsdp')
- key_weight_grad: float32 [1152, 1152], P('fsdp')
- value_weight_grad: float32 [1152, 1152], P('fsdp')
- query_bias_grad: float32 [1152], P('fsdp')
- value_bias_grad: float32 [1152], P('fsdp')
- out_weight_grad: float32 [1152, 1152], P('fsdp')
- out_bias_grad: float32 [1152], P('fsdp')
- mlp_gain_grad: float32 [1152], P('fsdp')
- mlp_shift_grad: float32 [1152], P('fsdp')
- inner_weight_grad: float32 [1152, 4304], P('fsdp')
- inner_bias_grad: float32 [4304], P('fsdp')
- outer_weight_grad: float32 [4304, 1152], P('fsdp')
- outer_bias_grad: float32 [1152], P('fsdp')
Inputs may be any that keep to these rules, and one draw needn't show every extreme that they name: `key_mask`: each image's row is 1 on its first positions and 0 after them; at least 128 positions are 1.
All inputs are finite; a program needn't handle non-finite values.
Results may differ from a plain program's by a relative error of at most 0.013.
The roundings to bfloat16 on the way count: a program that leaves them out, or rounds other values in their place, can miss the bound.
Values may be sent and summed in bfloat16 or wider, within the bound.
A program may use at most 256 MiB of HBM per device.

v0:
```python
import jax
import jax.numpy as jnp
from jax import lax
from jax.sharding import PartitionSpec as P

HD = 72
EPSILON = 1e-06
MASKED = -1e30


def product(left, right):
    return jnp.dot(left, right, preferred_element_type=jnp.float32)


def product_rows(left, right):
    return lax.dot_general(
        left, right, (((0,), (0,)), ((), ())), preferred_element_type=jnp.float32
    )


def product_back(left, right):
    return lax.dot_general(
        left, right, (((1,), (1,)), ((), ())), preferred_element_type=jnp.float32
    )


def gelu_tanh(values):
    return jax.nn.gelu(values, approximate=True)


def normalize(values):
    center = values - jnp.mean(values, axis=-1, keepdims=True)
    factor = lax.rsqrt(jnp.mean(center * center, axis=-1, keepdims=True) + EPSILON)
    return (center * factor, factor)


def norm_back(grad_normed, normed, factor):
    first = jnp.mean(grad_normed, axis=-1, keepdims=True)
    second = jnp.mean(grad_normed * normed, axis=-1, keepdims=True)
    return factor * (grad_normed - first - normed * second)


def forward_image(items):
    query, keys, values, valid = items
    length, local = query.shape
    heads = local // HD
    scale = HD ** (-0.5)
    block = min(512, length)
    key_three = keys.reshape(length, heads, HD)
    value_three = values.reshape(length, heads, HD)
    blocks = query.reshape(length // block, block, heads, HD)

    def forward_visit(query_block):
        scores = (
            jnp.einsum("qhd,khd->hqk", query_block, key_three, preferred_element_type=jnp.float32)
            * scale
        )
        scores = jnp.where(valid[None, None, :], scores, MASKED)
        highest = jnp.max(scores, axis=-1, keepdims=True)
        logsum = highest + jnp.log(jnp.sum(jnp.exp(scores - highest), axis=-1, keepdims=True))
        attention = jnp.exp(scores - logsum).astype(jnp.bfloat16)
        attended = jnp.einsum(
            "hqk,khd->qhd", attention, value_three, preferred_element_type=jnp.float32
        )
        return (attended.astype(jnp.bfloat16), logsum[..., 0])

    attended, logsum = lax.map(forward_visit, blocks)
    return (attended.reshape(length, local), logsum)


def backward_image(items):
    query, keys, values, attended, grad_out, logsum, valid = items
    length, local = query.shape
    heads = local // HD
    scale = HD ** (-0.5)
    block = min(512, length)
    count_blocks = length // block
    key_three = keys.reshape(length, heads, HD)
    value_three = values.reshape(length, heads, HD)
    blocks = (
        query.reshape(count_blocks, block, heads, HD),
        attended.reshape(count_blocks, block, heads, HD),
        grad_out.reshape(count_blocks, block, heads, HD),
        logsum,
    )
    zeros = jnp.zeros((length, heads, HD), jnp.float32)

    def backward_visit(carry, piece):
        query_block, out_block, grad_block, logsum_block = piece
        grad_keys, grad_values = carry
        scores = (
            jnp.einsum("qhd,khd->hqk", query_block, key_three, preferred_element_type=jnp.float32)
            * scale
        )
        scores = jnp.where(valid[None, None, :], scores, MASKED)
        chance = jnp.exp(scores - logsum_block[:, :, None])
        chance_low = chance.astype(jnp.bfloat16)
        grad_values = grad_values + jnp.einsum(
            "hqk,qhd->khd", chance_low, grad_block, preferred_element_type=jnp.float32
        )
        grad_chance = jnp.einsum(
            "qhd,khd->hqk", grad_block, value_three, preferred_element_type=jnp.float32
        )
        delta = jnp.sum(grad_block.astype(jnp.float32) * out_block.astype(jnp.float32), axis=-1).T
        grad_scores = (chance * (grad_chance - delta[:, :, None]) * scale).astype(jnp.bfloat16)
        grad_query = jnp.einsum(
            "hqk,khd->qhd", grad_scores, key_three, preferred_element_type=jnp.float32
        )
        grad_keys = grad_keys + jnp.einsum(
            "hqk,qhd->khd", grad_scores, query_block, preferred_element_type=jnp.float32
        )
        return ((grad_keys, grad_values), grad_query.astype(jnp.bfloat16))

    (grad_keys, grad_values), grad_query = lax.scan(backward_visit, (zeros, zeros), blocks)
    return (
        grad_query.reshape(length, local),
        grad_keys.astype(jnp.bfloat16).reshape(length, local),
        grad_values.astype(jnp.bfloat16).reshape(length, local),
    )


def shards(
    images,
    key_mask,
    attn_gain,
    attn_shift,
    query_weight,
    key_weight,
    value_weight,
    query_bias,
    value_bias,
    out_weight,
    out_bias,
    mlp_gain,
    mlp_shift,
    inner_weight,
    inner_bias,
    outer_weight,
    outer_bias,
    cotangent,
):
    gathered = (
        lax.all_gather(attn_gain, "fsdp", axis=0, tiled=True),
        lax.all_gather(attn_shift, "fsdp", axis=0, tiled=True),
        lax.all_gather(query_weight, "fsdp", axis=0, tiled=True),
        lax.all_gather(key_weight, "fsdp", axis=0, tiled=True),
        lax.all_gather(value_weight, "fsdp", axis=0, tiled=True),
        lax.all_gather(query_bias, "fsdp", axis=0, tiled=True),
        lax.all_gather(value_bias, "fsdp", axis=0, tiled=True),
        lax.all_gather(out_weight, "fsdp", axis=0, tiled=True),
        lax.all_gather(out_bias, "fsdp", axis=0, tiled=True),
        lax.all_gather(mlp_gain, "fsdp", axis=0, tiled=True),
        lax.all_gather(mlp_shift, "fsdp", axis=0, tiled=True),
        lax.all_gather(inner_weight, "fsdp", axis=0, tiled=True),
        lax.all_gather(inner_bias, "fsdp", axis=0, tiled=True),
        lax.all_gather(outer_weight, "fsdp", axis=0, tiled=True),
        lax.all_gather(outer_bias, "fsdp", axis=0, tiled=True),
    )
    (
        gain_attn,
        shift_attn,
        w_query,
        w_key,
        w_value,
        b_query,
        b_value,
        w_out,
        b_out,
        gain_mlp,
        shift_mlp,
        w_inner,
        b_inner,
        w_outer,
        b_outer,
    ) = gathered
    count, block_len, width = images.shape
    rows = count * block_len
    flat = images.reshape(rows, width).astype(jnp.float32)
    normed_one, factor_one = normalize(flat)
    hidden_one = (
        normed_one * gain_attn.astype(jnp.float32) + shift_attn.astype(jnp.float32)
    ).astype(jnp.bfloat16)
    query = (product(hidden_one, w_query) + b_query.astype(jnp.float32)).astype(jnp.bfloat16)
    keys = product(hidden_one, w_key).astype(jnp.bfloat16)
    values = (product(hidden_one, w_value) + b_value.astype(jnp.float32)).astype(jnp.bfloat16)
    query_heads, key_heads, value_heads = (
        lax.all_to_all(
            query.reshape(count, block_len, width), "seq", split_axis=2, concat_axis=1, tiled=True
        ),
        lax.all_to_all(
            keys.reshape(count, block_len, width), "seq", split_axis=2, concat_axis=1, tiled=True
        ),
        lax.all_to_all(
            values.reshape(count, block_len, width), "seq", split_axis=2, concat_axis=1, tiled=True
        ),
    )
    valid = key_mask > 0
    attended, logsum = lax.map(forward_image, (query_heads, key_heads, value_heads, valid))
    attended_tokens = lax.all_to_all(attended, "seq", split_axis=1, concat_axis=2, tiled=True)
    attended_flat = attended_tokens.reshape(rows, width)
    second = flat + product(attended_flat, w_out) + b_out.astype(jnp.float32)
    normed_two, factor_two = normalize(second)
    hidden_two = (normed_two * gain_mlp.astype(jnp.float32) + shift_mlp.astype(jnp.float32)).astype(
        jnp.bfloat16
    )
    inner = product(hidden_two, w_inner) + b_inner.astype(jnp.float32)
    active = gelu_tanh(inner).astype(jnp.bfloat16)
    layer_out = second + product(active, w_outer) + b_outer.astype(jnp.float32)
    unpacked = (
        lax.all_gather(attn_gain, "fsdp", axis=0, tiled=True),
        lax.all_gather(attn_shift, "fsdp", axis=0, tiled=True),
        lax.all_gather(query_weight, "fsdp", axis=0, tiled=True),
        lax.all_gather(key_weight, "fsdp", axis=0, tiled=True),
        lax.all_gather(value_weight, "fsdp", axis=0, tiled=True),
        lax.all_gather(query_bias, "fsdp", axis=0, tiled=True),
        lax.all_gather(value_bias, "fsdp", axis=0, tiled=True),
        lax.all_gather(out_weight, "fsdp", axis=0, tiled=True),
        lax.all_gather(out_bias, "fsdp", axis=0, tiled=True),
        lax.all_gather(mlp_gain, "fsdp", axis=0, tiled=True),
        lax.all_gather(mlp_shift, "fsdp", axis=0, tiled=True),
        lax.all_gather(inner_weight, "fsdp", axis=0, tiled=True),
        lax.all_gather(inner_bias, "fsdp", axis=0, tiled=True),
        lax.all_gather(outer_weight, "fsdp", axis=0, tiled=True),
        lax.all_gather(outer_bias, "fsdp", axis=0, tiled=True),
    )
    (
        gain_attn,
        shift_attn,
        w_query,
        w_key,
        w_value,
        b_query,
        b_value,
        w_out,
        b_out,
        gain_mlp,
        shift_mlp,
        w_inner,
        b_inner,
        w_outer,
        b_outer,
    ) = unpacked
    upstream = cotangent.reshape(rows, width)
    grad_active = product_back(upstream, w_outer)
    grad_inner = jax.vjp(gelu_tanh, inner)[1](grad_active)[0]
    grad_inner_low = grad_inner.astype(jnp.bfloat16)
    grad_hidden_two = product_back(grad_inner_low, w_inner)
    grad_second = upstream.astype(jnp.float32) + norm_back(
        grad_hidden_two * gain_mlp.astype(jnp.float32), normed_two, factor_two
    )
    mlp_terms = (
        jnp.sum(grad_hidden_two * normed_two, axis=0),
        jnp.sum(grad_hidden_two, axis=0),
        product_rows(hidden_two, grad_inner_low),
        jnp.sum(grad_inner, axis=0),
        product_rows(active, upstream),
        jnp.sum(upstream.astype(jnp.float32), axis=0),
    )
    grad_second_low = grad_second.astype(jnp.bfloat16)
    grad_attended = product_back(grad_second_low, w_out).astype(jnp.bfloat16)
    grad_heads = lax.all_to_all(
        grad_attended.reshape(count, block_len, width),
        "seq",
        split_axis=2,
        concat_axis=1,
        tiled=True,
    )
    grad_query_heads, grad_key_heads, grad_value_heads = lax.map(
        backward_image, (query_heads, key_heads, value_heads, attended, grad_heads, logsum, valid)
    )
    grad_query, grad_keys, grad_values = (
        lax.all_to_all(grad_query_heads, "seq", split_axis=1, concat_axis=2, tiled=True),
        lax.all_to_all(grad_key_heads, "seq", split_axis=1, concat_axis=2, tiled=True),
        lax.all_to_all(grad_value_heads, "seq", split_axis=1, concat_axis=2, tiled=True),
    )
    grad_query = grad_query.reshape(rows, width)
    grad_keys = grad_keys.reshape(rows, width)
    grad_values = grad_values.reshape(rows, width)
    grad_hidden_one = (
        product_back(grad_query, w_query)
        + product_back(grad_keys, w_key)
        + product_back(grad_values, w_value)
    )
    images_grad = grad_second + norm_back(
        grad_hidden_one * gain_attn.astype(jnp.float32), normed_one, factor_one
    )
    attn_terms = (
        jnp.sum(grad_hidden_one * normed_one, axis=0),
        jnp.sum(grad_hidden_one, axis=0),
        product_rows(hidden_one, grad_query),
        product_rows(hidden_one, grad_keys),
        product_rows(hidden_one, grad_values),
        jnp.sum(grad_query.astype(jnp.float32), axis=0),
        jnp.sum(grad_values.astype(jnp.float32), axis=0),
        product_rows(attended_flat, grad_second_low),
        jnp.sum(grad_second, axis=0),
    )
    shard_grads = (
        lax.psum_scatter(attn_terms[0], "fsdp", scatter_dimension=0, tiled=True),
        lax.psum_scatter(attn_terms[1], "fsdp", scatter_dimension=0, tiled=True),
        lax.psum_scatter(attn_terms[2], "fsdp", scatter_dimension=0, tiled=True),
        lax.psum_scatter(attn_terms[3], "fsdp", scatter_dimension=0, tiled=True),
        lax.psum_scatter(attn_terms[4], "fsdp", scatter_dimension=0, tiled=True),
        lax.psum_scatter(attn_terms[5], "fsdp", scatter_dimension=0, tiled=True),
        lax.psum_scatter(attn_terms[6], "fsdp", scatter_dimension=0, tiled=True),
        lax.psum_scatter(attn_terms[7], "fsdp", scatter_dimension=0, tiled=True),
        lax.psum_scatter(attn_terms[8], "fsdp", scatter_dimension=0, tiled=True),
        lax.psum_scatter(mlp_terms[0], "fsdp", scatter_dimension=0, tiled=True),
        lax.psum_scatter(mlp_terms[1], "fsdp", scatter_dimension=0, tiled=True),
        lax.psum_scatter(mlp_terms[2], "fsdp", scatter_dimension=0, tiled=True),
        lax.psum_scatter(mlp_terms[3], "fsdp", scatter_dimension=0, tiled=True),
        lax.psum_scatter(mlp_terms[4], "fsdp", scatter_dimension=0, tiled=True),
        lax.psum_scatter(mlp_terms[5], "fsdp", scatter_dimension=0, tiled=True),
    )
    summed = lax.psum(
        (
            shard_grads[0],
            shard_grads[1],
            shard_grads[2],
            shard_grads[3],
            shard_grads[4],
            shard_grads[5],
            shard_grads[6],
            shard_grads[7],
            shard_grads[8],
            shard_grads[9],
            shard_grads[10],
            shard_grads[11],
            shard_grads[12],
            shard_grads[13],
            shard_grads[14],
        ),
        "seq",
    )
    return (
        layer_out.reshape(count, block_len, width),
        images_grad.reshape(count, block_len, width),
        summed[0],
        summed[1],
        summed[2],
        summed[3],
        summed[4],
        summed[5],
        summed[6],
        summed[7],
        summed[8],
        summed[9],
        summed[10],
        summed[11],
        summed[12],
        summed[13],
        summed[14],
    )


def solution(mesh):
    placed = (
        P("fsdp", "seq", None),
        P("fsdp", None),
        P("fsdp"),
        P("fsdp"),
        P("fsdp", None),
        P("fsdp", None),
        P("fsdp", None),
        P("fsdp"),
        P("fsdp"),
        P("fsdp", None),
        P("fsdp"),
        P("fsdp"),
        P("fsdp"),
        P("fsdp", None),
        P("fsdp"),
        P("fsdp", None),
        P("fsdp"),
        P("fsdp", "seq", None),
    )
    return jax.shard_map(
        shards,
        mesh=mesh,
        in_specs=placed,
        out_specs=(
            P("fsdp", "seq", None),
            P("fsdp", "seq", None),
            P("fsdp"),
            P("fsdp"),
            P("fsdp", None),
            P("fsdp", None),
            P("fsdp", None),
            P("fsdp"),
            P("fsdp"),
            P("fsdp", None),
            P("fsdp"),
            P("fsdp"),
            P("fsdp"),
            P("fsdp", None),
            P("fsdp"),
            P("fsdp", None),
            P("fsdp"),
        ),
        check_vma=False,
    )
```

profile of v0, /device:TPU:0, one launch (start us, length us, event | category | flops | bytes accessed | tf_op | source)
XLA Modules:
  0.0 1205.4 jit_solution(2965813202933017199)
XLA Ops:
  15.5 33.4 %all-reduce.23 = (bf16[1152]{0:T(1024)(128)(2,1)S(1)}, bf16[1152]{0:T(1024)(128)(2,1)S(1)}, bf16[1152]{0:T(1024)(128)(2,1)S(1)}, bf16[1152]{0:T(1024)(128)(2,1)S...) all-reduce(bf16[1152]{0:T(1024)(128)(2,1)S(1)} %dynamic-update-slic, ...), channel_id=1, replica_groups=mesh['seq'=4,'fsdp'=8] {'fsdp'}, use_global_device_ids=true, to_apply=%add.1 | all-reduce | flops 13520 | bytes 54080
  51.2 3.5 fusion.25
  54.6 2.0 copy.63
  56.6 3.6 all-to-all-start
  60.2 22.2 %all-gather.12.cloned.1.call-done = bf16[1152,1152]{1,0:T(8,128)(2,1)} async-done(((bf16[144,1152]{1,0:T(8,128)(2,1)}), bf16[1152,1152]{1,0:T(8,128)(2,1)}) %all-gather.12.cloned.1.call-update) | async-done | bytes 2654224 | tf_op jit(solution)/shard_map/all_gather | solution.py:146
  82.4 4.1 convolution_convert_fusion.3
  86.4 3.2 copy.69
  89.7 3.6 all-to-all-start.2
  93.3 23.8 %all-gather.10.cloned.1.call-done = bf16[1152,1152]{1,0:T(8,128)(2,1)} async-done(((bf16[144,1152]{1,0:T(8,128)(2,1)}), bf16[1152,1152]{1,0:T(8,128)(2,1)}) %all-gather.10.cloned.1.call-update) | async-done | bytes 2654224 | tf_op jit(solution)/shard_map/all_gather | solution.py:145
  117.2 4.4 fusion.26
  121.5 3.2 copy.66
  124.8 4.5 all-to-all-start.1
  130.6 14.4 %all-to-all-done.1 = bf16[3,128,1152]{1,0,2:T(4,128)(2,1)} async-done(((bf16[3,128,1152]{1,0,2:T(4,128)(2,1)}), bf16[3,128,1152]{1,0,2:T(4,128)(2,1)}, u32[]{:S(2)}, u32[]{:S(2)}) %all-to-all-start.1) | async-done | bytes 884768 | tf_op jit(solution)/shard_map/all_to_all | solution.py:187
  147.7 13.9 %while.10 = (s32[]{:T(128)}, bf16[3,512,288]{1,2,0:T(8,128)(2,1)}, f32[3,1,4,512]{3,2,1,0:T(4,128)}, bf16[3,512,288]{1,2,0:T(8,128)(2,1)S(1)}, pred[3,512]{1,0:T...) while((s32[]{:T(128)}, bf16[3,512,288]{1,2,0:T(8,128)(2,1)}, ...), condition=%wide.region_5.6_spmd, body=%wide.region_2.5_spmd.sunk | while | flops 313669632 | bytes 16190065 | solution.py:198
  161.5 3.5 copy.72
  165.0 4.3 all-to-all-start.3
  173.3 15.2 %all-to-all-done.3 = bf16[3,512,288]{2,0,1:T(4,128)(2,1)} async-done(((bf16[3,512,288]{2,0,1:T(4,128)(2,1)}), bf16[3,512,288]{2,0,1:T(4,128)(2,1)}, u32[]{:S(2)}, u32[]{:S(2)}) %all-to-all-start.3) | async-done | bytes 884768 | tf_op jit(solution)/shard_map/all_to_all | solution.py:199
  188.4 3.5 copy.99
  192.0 2.8 reshape.280
  194.8 3.6 fusion.42
  200.5 47.5 %all-gather.18.cloned.1.call-done = bf16[8,538,1152]{2,1,0:T(8,128)(2,1)} async-done(((bf16[1,538,1152]{2,1,0:T(8,128)(2,1)}), bf16[8,538,1152]{2,1,0:T(8,128)(2,1)}) %all-gather.18.cloned.1.call-update) | async-done | bytes 9916432 | tf_op jit(solution)/shard_map/all_gather | solution.py:156
  248.0 12.4 %reshape.318 = bf16[4304,1152]{1,0:T(8,128)(2,1)} reshape(bf16[8,538,1152]{2,1,0:T(8,128)(2,1)} %all-gather.18.cloned.1.call-done) | data formatting | bytes 19832832
  260.4 10.5 fusion.44
  270.9 72.6 %all-gather.16.cloned.1.call-done = bf16[1152,4304]{1,0:T(8,128)(2,1)} async-done(((bf16[144,4304]{1,0:T(8,128)(2,1)}), bf16[1152,4304]{1,0:T(8,128)(2,1)}) %all-gather.16.cloned.1.call-update) | async-done | bytes 9916432 | tf_op jit(solution)/shard_map/all_gather | solution.py:154
  343.5 20.9 %fusion.38 = (f32[4304]{0:T(1024)}, bf16[384,4304]{0,1:T(8,128)(2,1)S(1)}, f32[384,4304]{0,1:T(8,128)}) fusion(f32[384,4304]{0,1:T(8,128)} %fusion.44, f32[4304]{0:T(1024)} %convert_element_type.163, bf16[1152,4304]{1,0:T(8,128)(2,1)} %all-gather.16.cloned.1.call-done, f32[384,1152]{1,0:T(8,128)} %copy-done.1, f32[1152]{0:T(1024)} %convert_element_type.161, ...), kind=kOutput, calls=%fused_computation.108 | convolution fusion | flops 3846471424 | bytes 28259968 | tf_op jit(solution)/shard_map/dot_general | solution.py:12
  364.4 10.7 multiply_reduce_fusion
  377.7 4.0 fusion.32
  381.7 4.7 convolution_convert_fusion.2
  386.3 3.2 copy.74
  389.6 19.9 %all_to_all.132 = bf16[3,128,1152]{1,0,2:T(4,128)(2,1)S(1)} all-to-all(bf16[3,128,1152]{1,0,2:T(4,128)(2,1)} %copy.74), channel_id=1, replica_groups=mesh['seq'=4,'fsdp'=8] {'seq'}, dimensions={2} | all-to-all | bytes 1769472 | tf_op jit(solution)/shard_map/all_to_all | solution.py:261
  413.7 27.9 %while.27 = (s32[]{:T(128)}, bf16[3,512,288]{1,2,0:T(8,128)(2,1)}, bf16[3,512,288]{1,2,0:T(8,128)(2,1)}, bf16[3,512,288]{1,2,0:T(8,128)(2,1)}, bf16[3,512,288]{1...) while((s32[]{:T(128)}, bf16[3,512,288]{1,2,0:T(8,128)(2,1)}, ...), condition=%wide.region_12.13_spmd, body=%wide.region_10.12_spmd.sunk | while | flops 767539200 | bytes 27183264 | solution.py:268
  417.4 1.7 multiply_convert_fusion.5
  426.7 1.7 multiply_convert_fusion.5
  436.0 1.8 multiply_convert_fusion.5
  441.6 3.4 copy.77
  445.0 3.6 all-to-all-start.5
  449.0 18.1 %all-to-all-done.5 = bf16[3,512,288]{2,0,1:T(4,128)(2,1)S(1)} async-done(((bf16[3,512,288]{2,0,1:T(4,128)(2,1)}), bf16[3,512,288]{2,0,1:T(4,128)(2,1)S(1)}, u32[]{:S(2)}, u32[]{:S(2)}) %all-to-all-start.5) | async-done | bytes 884768 | tf_op jit(solution)/shard_map/all_to_all | solution.py:272
  467.2 2.8 convert_reduce_fusion.1
  470.0 2.1 reshape.284
  472.1 4.0 fusion.46
  476.1 2.8 copy.79
  478.9 21.9 %all_to_all.133 = bf16[3,512,288]{2,0,1:T(4,128)(2,1)S(1)} all-to-all(bf16[3,512,288]{2,0,1:T(4,128)(2,1)S(1)} %copy.79), channel_id=1, replica_groups=mesh['seq'=4,'fsdp'=8] {'seq'}, dimensions={1} | all-to-all | bytes 1769472 | tf_op jit(solution)/shard_map/all_to_all | solution.py:273
  503.7 5.2 fusion.47
  509.0 2.8 copy.81
  511.8 20.5 %all_to_all.134 = bf16[3,512,288]{2,0,1:T(4,128)(2,1)S(1)} all-to-all(bf16[3,512,288]{2,0,1:T(4,128)(2,1)S(1)} %copy.81), channel_id=1, replica_groups=mesh['seq'=4,'fsdp'=8] {'seq'}, dimensions={1} | all-to-all | bytes 1769472 | tf_op jit(solution)/shard_map/all_to_all | solution.py:274
  532.3 1.8 convert_reduce_fusion
  534.1 1.7 reshape.286
  535.8 5.2 fusion.48
  542.5 11.6 fusion.28
  555.3 15.7 %fusion.37 = f32[4304,1152]{1,0:T(8,128)} fusion(bf16[384,1152]{1,0:T(8,128)(2,1)S(1)} %bitcast.215, f32[384,4304]{0,1:T(8,128)} %get-tuple-element.275), kind=kOutput, calls=%fused_computation.107 | convolution fusion | flops 3822778368 | bytes 27328512 | tf_op jit(solution)/shard_map/dot_general | solution.py:16
  571.0 387.5 %fusion = f32[544,1152]{1,0:T(8,128)} fusion(f32[4304,1152]{1,0:T(8,128)} %fusion.37), kind=kCustom, calls=%all-reduce-scatter | all-reduce-scatter fusion | flops 5013505 | bytes 22340096
  960.1 2.0 collective-permute-start
  962.8 9.9 concatenate
  972.7 3.4 constant_dynamic-slice_fusion.8
  976.1 45.6 %reduce-scatter.16.cloned.1.call-done = f32[144,4304]{1,0:T(8,128)} async-done(((f32[1152,4304]{1,0:T(8,128)}), f32[144,4304]{1,0:T(8,128)}) %reduce-scatter.16.cloned.1.call-update) | async-done | bytes 2479120 | tf_op jit(solution)/shard_map/reduce_scatter | solution.py:310
  1023.9 11.6 fusion.24
  1037.6 3.4 fusion.45
  1043.6 2.9 multiply_reduce_fusion.1
  1046.5 29.1 %all-reduce.20 = (f32[1152]{0:T(1024)S(1)}, f32[1152]{0:T(1024)S(1)}, f32[1152]{0:T(1024)S(1)}, f32[1152]{0:T(1024)S(1)}, f32[1152]{0:T(1024)S(1)}, /*index=5*/f...) all-reduce(f32[1152]{0:T(1024)S(1)} %get-tuple-element.175, ...), channel_id=2, replica_groups=mesh['seq'=4,'fsdp'=8] {'fsdp'}, use_global_device_ids=true, to_apply=%region_16.17.clone | all-reduce | flops 13520 | bytes 108160
  1076.2 17.0 %all-reduce.21 = (f32[144]{0:T(256)}, f32[144]{0:T(256)}, f32[144]{0:T(256)}, f32[144]{0:T(256)}, f32[144]{0:T(256)}, /*index=5*/f32[144]{0:T(256)}, f32[144]{0:T(256)}, f32[538]{0:T(1024)}, f32[144]{0:T(256)}) all-reduce(f32[144]{0:T(256)S(1)} %dynamic-slice.10, ...), channel_id=1, replica_groups=mesh['seq'=4,'fsdp'=8] {'seq'}, use_global_device_ids=true, to_apply=%region_17.18 | all-reduce | flops 1690 | bytes 13520 | tf_op jit(solution)/shard_map/psum | solution.py:315
  1093.2 3.3 multiply_add_fusion
  1096.5 91.7 %all-reduce.26.cloned.1.call-done = (f32[144,1152]{1,0:T(8,128)}, f32[144,1152]{1,0:T(8,128)}, f32[144,1152]{1,0:T(8,128)}, f32[144,1152]{1,0:T(8,128)}, f32[144,4304]{1,0:T(8,128)}, /*index=5*/f32[538,1152]{1,0:T(8,128)}) async-done(((f32[144,1152]{1,0:T(8,128)}, f32[144,1152]{1,0:T(8,128)}, f32[144,1152]{1,0:T(8,128)}, f32[144,1152]{1,0:T(8,128)}, f32[144,4304]{1,0:T(8,128)}, ...) | async-done | bytes 7612432 | tf_op jit(solution)/shard_map/psum | solution.py:315
  1188.2 2.1 copy.145
  1190.4 2.0 copy.146
  (282 shorter events, 81.7 us)
Async XLA Ops:
  7.2 4.1 copy-start.41
  7.2 6.0 copy-start.46
  7.2 6.2 copy-start.47
  7.2 6.5 copy-start.48
  7.2 6.7 copy-start.49
  7.2 7.0 copy-start.50
  7.3 7.2 copy-start.51
  7.3 7.5 copy-start.52
  7.3 7.7 copy-start.53
  7.3 7.9 copy-start.43
  7.3 41.6 %copy-start = (bf16[3,128,1152]{2,1,0:T(8,128)(2,1)S(1)}, bf16[3,128,1152]{2,1,0:T(8,128)(2,1)}, u32[]{:S(2)}) copy-start(bf16[3,128,1152]{2,1,0:T(8,128)(2,1)} %param.22) | copy-start | bytes 2654212
  7.3 43.8 %all-gather.8.cloned.1.call-start = ((), (), s32[]{:S(2)}) async-start(), calls=%async_computation.13 | async-start | bytes 2985984 | tf_op jit(solution)/shard_map/all_gather | solution.py:147
  8.0 74.3 %all-gather.12.cloned.1.call-start = ((), (), s32[]{:S(2)}) async-start(), calls=%async_computation.15 | async-start | bytes 2985984 | tf_op jit(solution)/shard_map/all_gather | solution.py:146
  8.8 108.4 %all-gather.10.cloned.1.call-start = ((), (), s32[]{:S(2)}) async-start(), calls=%async_computation.14 | async-start | bytes 2985984 | tf_op jit(solution)/shard_map/all_gather | solution.py:145
  9.5 185.3 %all-gather.14.cloned.1.call-start = ((), (), s32[]{:S(2)}) async-start(), calls=%async_computation.16 | async-start | bytes 2985984 | tf_op jit(solution)/shard_map/all_gather | solution.py:150
  10.1 237.9 %all-gather.18.cloned.1.call-start = ((), (), s32[]{:S(2)}) async-start(), calls=%async_computation.23 | async-start | bytes 11280384 | tf_op jit(solution)/shard_map/all_gather | solution.py:156
  10.7 332.8 %all-gather.16.cloned.1.call-start = ((), (), s32[]{:S(2)}) async-start(), calls=%async_computation.17 | async-start | bytes 11280384 | tf_op jit(solution)/shard_map/all_gather | solution.py:154
  51.1 31.3 %copy-start.17 = (bf16[384,1152]{1,0:T(8,128)(2,1)}, bf16[384,1152]{1,0:T(8,128)(2,1)S(1)}, u32[]{:S(2)}) copy-start(bf16[384,1152]{1,0:T(8,128)(2,1)S(1)} %add_convert_fusion.2) | copy-start | bytes 2654212
  56.6 33.1 %all-to-all-start = ((bf16[3,128,1152]{1,0,2:T(4,128)(2,1)}), bf16[3,128,1152]{1,0,2:T(4,128)(2,1)S(1)}, u32[]{:S(2)}, u32[]{:S(2)}) async-start(bf16[3,128,1152]{1,0,2:T(4,128)(2,1)} %copy.63), calls=%async_computation | async-start | bytes 2359296 | tf_op jit(solution)/shard_map/all_to_all | solution.py:193
  89.7 35.1 %all-to-all-start.2 = ((bf16[3,128,1152]{1,0,2:T(4,128)(2,1)}), bf16[3,128,1152]{1,0,2:T(4,128)(2,1)S(1)}, u32[]{:S(2)}, u32[]{:S(2)}) async-start(bf16[3,128,1152]{1,0,2:T(4,128)(2,1)} %copy.69), calls=%async_computation.2 | async-start | bytes 2359296 | tf_op jit(solution)/shard_map/all_to_all | solution.py:190
  121.5 7.8 copy-start.38
  124.8 20.2 %all-to-all-start.1 = ((bf16[3,128,1152]{1,0,2:T(4,128)(2,1)}), bf16[3,128,1152]{1,0,2:T(4,128)(2,1)}, u32[]{:S(2)}, u32[]{:S(2)}) async-start(bf16[3,128,1152]{1,0,2:T(4,128)(2,1)} %copy.66), calls=%async_computation.1 | async-start | bytes 2359296 | tf_op jit(solution)/shard_map/all_to_all | solution.py:187
  145.0 1.5 copy-start.13
  165.0 23.4 %all-to-all-start.3 = ((bf16[3,512,288]{2,0,1:T(4,128)(2,1)}), bf16[3,512,288]{2,0,1:T(4,128)(2,1)}, u32[]{:S(2)}, u32[]{:S(2)}) async-start(bf16[3,512,288]{2,0,1:T(4,128)(2,1)} %copy.72), calls=%async_computation.3 | async-start | bytes 3145728 | tf_op jit(solution)/shard_map/all_to_all | solution.py:199
  169.3 806.7 %reduce-scatter.14.cloned.1.call-start = ((), (), s32[]{:S(2)}) async-start(), calls=%async_computation.21 | async-start | bytes 5971968 | tf_op jit(solution)/shard_map/reduce_scatter | solution.py:306
  198.4 1.2 copy-start.1
  343.5 20.9 %copy-start.2 = (f32[384,1152]{1,0:T(8,128)S(1)}, f32[384,1152]{1,0:T(8,128)}, u32[]{:S(2)}) copy-start(f32[384,1152]{1,0:T(8,128)} %copy-done.1) | copy-start | bytes 5308420
  343.5 20.9 %copy-start.26 = (f32[384]{0:T(512)S(1)}, f32[384]{0:T(512)}, u32[]{:S(2)}) copy-start(f32[384]{0:T(512)} %add_rsqrt_fusion) | copy-start | bytes 4612
  364.4 10.7 copy-start.14
  364.4 10.7 copy-start.6
  375.1 2.5 copy-start.8
  441.6 7.0 copy-start.21
  441.6 7.0 copy-start.25
  441.6 7.0 copy-start.36
  441.6 7.0 copy-start.37
  445.0 22.2 %all-to-all-start.5 = ((bf16[3,512,288]{2,0,1:T(4,128)(2,1)}), bf16[3,512,288]{2,0,1:T(4,128)(2,1)S(1)}, u32[]{:S(2)}, u32[]{:S(2)}) async-start(bf16[3,512,288]{2,0,1:T(4,128)(2,1)} %copy.77), calls=%async_computation.5 | async-start | bytes 3145728 | tf_op jit(solution)/shard_map/all_to_all | solution.py:272
  448.5 527.5 %reduce-scatter.8.cloned.1.call-start = ((), (), s32[]{:S(2)}) async-start(), calls=%async_computation.18 | async-start | bytes 5971968 | tf_op jit(solution)/shard_map/reduce_scatter | solution.py:301
  472.1 4.0 copy-start.9
  476.1 500.0 %reduce-scatter.10.cloned.1.call-start = ((), (), s32[]{:S(2)}) async-start(), calls=%async_computation.19 | async-start | bytes 5971968 | tf_op jit(solution)/shard_map/reduce_scatter | solution.py:302
  508.9 467.2 %reduce-scatter.12.cloned.1.call-start = ((), (), s32[]{:S(2)}) async-start(), calls=%async_computation.20 | async-start | bytes 5971968 | tf_op jit(solution)/shard_map/reduce_scatter | solution.py:303
  541.0 1.5 copy-start.3
  541.0 1.5 copy-start.23
  541.0 1.5 copy-start.27
  541.0 480.7 %reduce-scatter.16.cloned.1.call-start = ((), (), s32[]{:S(2)}) async-start(), calls=%async_computation.22 | async-start | bytes 22560768 | tf_op jit(solution)/shard_map/reduce_scatter | solution.py:310
  554.1 634.1 %all-reduce.26.cloned.1.call-start = ((), (), s32[]{:S(2)}) async-start(), calls=%async_computation.24 | async-start | bytes 15335424 | tf_op jit(solution)/shard_map/psum | solution.py:315
  960.1 2.7 collective-permute-start
  1023.9 13.8 %copy-start.10 = (bf16[384,1152]{1,0:T(8,128)(2,1)S(1)}, bf16[384,1152]{1,0:T(8,128)(2,1)}, u32[]{:S(2)}) copy-start(bf16[384,1152]{1,0:T(8,128)(2,1)} %copy-done.9) | copy-start | bytes 2654212
  1037.6 3.4 copy-start.11
  1037.6 3.4 copy-start.45
  1041.0 1.5 copy-start.12
  1041.0 1.5 copy-start.22
  1041.0 1.5 copy-start.32
  1041.0 1.5 copy-start.34
  1041.1 2.5 copy-start.44
  1043.5 2.9 copy-start.28
  1043.5 3.0 copy-start.29
  1043.5 3.0 copy-start.30
  1043.5 3.0 copy-start.39
  1043.5 3.0 copy-start.40
  1043.5 49.7 %copy-start.5 = (f32[384,1152]{1,0:T(8,128)S(1)}, f32[384,1152]{1,0:T(8,128)}, u32[]{:S(2)}) copy-start(f32[384,1152]{1,0:T(8,128)} %copy-done.4) | copy-start | bytes 5308420
  1188.2 4.1 copy-start.19
  1188.2 4.9 copy-start.18
  1188.2 5.8 copy-start.16
  1194.0 2.6 copy-start.15
  (8 other events, 8.0 us)
Sparse Core Ops, SparseCore 0:
  9.8 37.7 all-gather.7
  49.1 33.1 all-gather.11
  84.0 33.0 all-gather.9
  118.6 33.0 all-gather.13
  153.3 94.6 all-gather.17
  249.5 93.9 all-gather.15
  381.8 58.8 reduce-scatter.13
  476.2 57.8 reduce-scatter.7
  536.4 74.3 reduce-scatter.9
  612.9 111.5 reduce-scatter.11
  726.9 294.8 reduce-scatter.15
  1026.6 161.5 all-reduce.25
where the time goes:
time: 1210 us
  blocking collectives  529 us (44%)
  waiting for transfers between devices  355 us (29%)
  matrix products  148 us (12%)
  local copies, waits for them, and re-layouts  111 us (9%)
  starting transfers between devices  22.1 us (2%)
  other arithmetic  21 us (2%)
  between operations  18.5 us (2%)
    unnamed x3, blocking collectives  450 us
    psum x1, waiting for transfers between devices, shards(): lax.psum((shard_grads[0], shard_grads[1], shard_grads[2], shard_grads[3],...  91.7 us
    all_gather x1, waiting for transfers between devices, shards(): lax.all_gather(inner_weight, 'fsdp', axis=0, tiled=True)  72.6 us
    dot_general x6, matrix products, product(): return jnp.dot(left, right, preferred_element_type=jnp.float32)  48 us
    unnamed x146, local copies, waits for them, and re-layouts  47.9 us
    all_gather x1, waiting for transfers between devices, shards(): lax.all_gather(outer_weight, 'fsdp', axis=0, tiled=True)  47.5 us
    dot_general x6, matrix products, product_rows(): lax.dot_general(left, right, (((0,), (0,)), ((), ())), preferred_element_...  45.7 us
    reduce_scatter x1, waiting for transfers between devices, shards(): lax.psum_scatter(mlp_terms[2], 'fsdp', scatter_dimension=0, tiled=True)  45.6 us
  transfers between devices with their start and end apart: 18, of which 10 were waited for; matrix products, arithmetic and copies ran while one was open for 51% of the time, Pallas kernels for 0%

commit v1 on v0

--- a/solution.py
+++ b/solution.py
@@ -139,6 +139,26 @@
     outer_bias,
     cotangent,
 ):
+
+    def scan_row_on(payload):
+        axis_id = "fsdp"
+        n_blocks = jax.lax.axis_size(axis_id)
+        block_out = map(lambda dd: (dd, (dd + 1) % n_blocks), range(n_blocks))
+        aux = range(n_blocks)
+        pages = list(block_out)
+        frames = list(map(lambda dd: (dd, (dd - 1) % n_blocks), aux))
+        res, spare = ([payload], [payload])
+        for _ in range(n_blocks // 2):
+            res.append(jax.lax.ppermute(res[-1], axis_name=axis_id, perm=pages))
+        m = 0
+        while m < (n_blocks - 1) // 2:
+            spare.append(jax.lax.ppermute(spare[-1], axis_name=axis_id, perm=frames))
+            m += 1
+        side_arr = jnp.concatenate([*res[::-1], *spare[1:]], axis=0)
+        return jnp.roll(
+            side_arr, (jax.lax.axis_index(axis_id) - n_blocks // 2) * payload.shape[0], axis=0
+        )
+
     gathered = (
         lax.all_gather(attn_gain, "fsdp", axis=0, tiled=True),
         lax.all_gather(attn_shift, "fsdp", axis=0, tiled=True),
@@ -151,7 +171,7 @@
         lax.all_gather(out_bias, "fsdp", axis=0, tiled=True),
         lax.all_gather(mlp_gain, "fsdp", axis=0, tiled=True),
         lax.all_gather(mlp_shift, "fsdp", axis=0, tiled=True),
-        lax.all_gather(inner_weight, "fsdp", axis=0, tiled=True),
+        scan_row_on(inner_weight),
         lax.all_gather(inner_bias, "fsdp", axis=0, tiled=True),
         lax.all_gather(outer_weight, "fsdp", axis=0, tiled=True),
         lax.all_gather(outer_bias, "fsdp", axis=0, tiled=True),

time: 1210 us -> 1240 us (1.025)
  waiting for transfers between devices: 355 us -> 284 us
  blocking collectives: 529 us -> 576 us
  local copies, waits for them, and re-layouts: 111 us -> 143 us
  starting transfers between devices: 22.1 us -> 47.9 us
    ppermute x0 -> x7, waiting for transfers between devices: none -> 68.8 us  [the longest x4 68.7 us: scan_row_on(): res.append(jax.lax.ppermute(res[-1], axis_name=axis_id, perm=pages))]
    all_gather x1, waiting for transfers between devices: 47.5 us -> 0.01 us  [shards(): lax.all_gather(outer_weight, 'fsdp', axis=0, tiled=True)]
    unnamed x3, blocking collectives: 450 us -> 496 us
    all_gather x1, waiting for transfers between devices: 72.6 us -> 32.9 us  [shards(): lax.all_gather(inner_weight, 'fsdp', axis=0, tiled=True)]
    unnamed x146 -> x183, local copies, waits for them, and re-layouts: 47.9 us -> 74 us
    ppermute x0 -> x7, starting transfers between devices: none -> 24.1 us  [the longest x4 15 us: scan_row_on(): res.append(jax.lax.ppermute(res[-1], axis_name=axis_id, perm=pages))]
    all_gather x1, waiting for transfers between devices: 23.8 us -> 0.01 us  [shards(): lax.all_gather(query_weight, 'fsdp', axis=0, tiled=True)]
    all_gather x1, waiting for transfers between devices: 22.2 us -> 0.02 us  [shards(): lax.all_gather(key_weight, 'fsdp', axis=0, tiled=True)]
  transfers between devices with their start and end apart: 18 -> 25, of which waited for: 10 -> 12; matrix products, arithmetic and copies ran while one was open for 51% -> 54% of each run, Pallas kernels for 0% -> 0%
where the time goes in v1:
time: 1240 us; the launch traced here: 1230 us
  blocking collectives  576 us (46%)
  waiting for transfers between devices  284 us (23%)
  matrix products  145 us (12%)
  local copies, waits for them, and re-layouts  143 us (12%)
  starting transfers between devices  47.9 us (4%)
  other arithmetic  19.9 us (2%)
  between operations  18.6 us (2%)
    unnamed x3, blocking collectives  496 us
    psum x1, waiting for transfers between devices, shards(): lax.psum((shard_grads[0], shard_grads[1], shard_grads[2], shard_grads[3],...  92.1 us
    unnamed x183, local copies, waits for them, and re-layouts  74 us
    ppermute x4, waiting for transfers between devices, scan_row_on(): res.append(jax.lax.ppermute(res[-1], axis_name=axis_id, perm=pages))  68.7 us
    reduce_scatter x1, waiting for transfers between devices, shards(): lax.psum_scatter(mlp_terms[2], 'fsdp', scatter_dimension=0, tiled=True)  45.8 us
    dot_general x6, matrix products, product(): return jnp.dot(left, right, preferred_element_type=jnp.float32)  45.7 us
    dot_general x6, matrix products, product_rows(): lax.dot_general(left, right, (((0,), (0,)), ((), ())), preferred_element_...  45.6 us
    all_gather x1, waiting for transfers between devices, shards(): lax.all_gather(inner_weight, 'fsdp', axis=0, tiled=True)  32.9 us
  transfers between devices with their start and end apart: 25, of which 12 were waited for; matrix products, arithmetic and copies ran while one was open for 54% of the time, Pallas kernels for 0%

profile of v1, /device:TPU:0, one launch (start us, length us, event | category | flops | bytes accessed | tf_op | source)
XLA Modules:
  0.0 1234.3 jit_solution(7012619822541522138)
XLA Ops:
  11.3 30.1 %collective-permute-done = bf16[144,4304]{1,0:T(8,128)(2,1)S(1)} collective-permute-done((bf16[144,4304]{1,0:T(8,128)(2,1)}, bf16[144,4304]{1,0:T(8,128)(2,1)S(1)}, u32[]{:S(2)}, u32[]{:S(2)}) %collective-permute-start) | collective-permute-done | bytes 1239584 | tf_op jit(solution)/shard_map/ppermute | solution.py:152
  45.0 26.9 %collective-permute-done.1 = bf16[144,4304]{1,0:T(8,128)(2,1)} collective-permute-done((bf16[144,4304]{1,0:T(8,128)(2,1)S(1)}, bf16[144,4304]{1,0:T(8,128)(2,1)}, u32[]{:S(2)}, u32[]{:S(2)}) %collective-permute-start.1) | collective-permute-done | bytes 1239584 | tf_op jit(solution)/shard_map/ppermute | solution.py:152
  71.8 12.9 %collective-permute-start.2 = (bf16[144,4304]{1,0:T(8,128)(2,1)}, bf16[144,4304]{1,0:T(8,128)(2,1)}, u32[]{:S(2)}, u32[]{:S(2)}) collective-permute-start(bf16[144,4304]{1,0:T(8,128)(2,1)} %collective-permute-done.1), channel_id=1, source_target_pairs={{0,1},{1,2},{2,3},{3,4},{4,5},{5,6},{6,7},{7,0},{8,9},{9,10},{10,1... | collective-permute-start | bytes 3718664 | tf_op jit(solution)/shard_map/ppermute | solution.py:152
  85.0 3.7 collective-permute-start.5
  92.9 79.3 %all-reduce.23 = (bf16[1152]{0:T(1024)(128)(2,1)S(1)}, bf16[1152]{0:T(1024)(128)(2,1)S(1)}, bf16[1152]{0:T(1024)(128)(2,1)S(1)}, bf16[1152]{0:T(1024)(128)(2,1)S...) all-reduce(bf16[1152]{0:T(1024)(128)(2,1)S(1)} %dynamic-update-slic, ...), channel_id=1, replica_groups=mesh['seq'=4,'fsdp'=8] {'fsdp'}, use_global_device_ids=true, to_apply=%add.1 | all-reduce | flops 13520 | bytes 54080
  176.4 3.5 collective-permute-start.6
  179.9 4.4 fusion.31
  184.3 3.3 copy.66
  187.6 4.3 all-to-all-start.1
  192.0 4.1 convolution_convert_fusion.3
  196.1 3.2 copy.69
  199.3 4.1 fusion.30
  203.4 3.4 copy.63
  206.8 11.7 collective-permute-done.3
  218.5 2.5 constant_dynamic-update-slice_fusion.19
  221.0 2.6 constant_dynamic-update-slice_fusion.18
  223.6 2.5 constant_dynamic-update-slice_fusion.17
  230.8 2.5 constant_dynamic-update-slice_fusion.12
  235.7 2.5 constant_dynamic-update-slice_fusion.10
  238.2 4.4 all-to-all-start
  246.1 11.3 all-to-all-done
  257.5 4.7 all-to-all-start.2
  268.4 4.0 all-to-all-done.2
  275.1 13.8 %while.10 = (s32[]{:T(128)}, bf16[3,512,288]{1,2,0:T(8,128)(2,1)}, f32[3,1,4,512]{3,2,1,0:T(4,128)}, bf16[3,512,288]{1,2,0:T(8,128)(2,1)S(1)}, pred[3,512]{1,0:T...) while((s32[]{:T(128)}, bf16[3,512,288]{1,2,0:T(8,128)(2,1)}, ...), condition=%wide.region_5.6_spmd, body=%wide.region_2.5_spmd.sunk | while | flops 313669632 | bytes 16191073 | solution.py:218
  288.9 3.4 copy.72
  292.3 4.4 all-to-all-start.3
  301.5 7.4 all-to-all-done.3
  308.9 3.5 copy.99
  312.5 2.8 reshape.280
  315.3 3.5 fusion.48
  320.9 11.8 reshape.318
  332.8 9.1 fusion.50
  341.9 18.0 %fusion.44 = (f32[4304]{0:T(1024)}, bf16[384,4304]{0,1:T(8,128)(2,1)}, f32[384,4304]{0,1:T(8,128)}) fusion(f32[384,4304]{0,1:T(8,128)S(1)} %fusion.50, f32[4304]{0:T(1024)S(1)} %copy-done.40, bf16[2304,4304]{1,0:T(8,128)(2,1)} %constant_dynamic-update-slice_fusion.4, s32[]{:T(128)S(6)} %select_n.23, f32[384,1152]{1,0:T(8,128)S(1)} %copy-done.2, ...), kind=kOutput, calls=%fused_computation.127 | convolution fusion | flops 3846471424 | bytes 28370564 | tf_op jit(solution)/shard_map/dot_general | solution.py:12
  359.9 32.9 %all-gather.16.cloned.1.call-done = bf16[1152,4304]{1,0:T(8,128)(2,1)} async-done(((bf16[144,4304]{1,0:T(8,128)(2,1)}), bf16[1152,4304]{1,0:T(8,128)(2,1)}) %all-gather.16.cloned.1.call-update) | async-done | bytes 9916432 | tf_op jit(solution)/shard_map/all_gather | solution.py:241
  392.8 11.1 multiply_reduce_fusion
  406.4 4.0 fusion.37
  410.4 4.7 convolution_convert_fusion.2
  415.1 3.2 copy.74
  418.3 20.1 %all_to_all.132 = bf16[3,128,1152]{1,0,2:T(4,128)(2,1)S(1)} all-to-all(bf16[3,128,1152]{1,0,2:T(4,128)(2,1)} %copy.74), channel_id=1, replica_groups=mesh['seq'=4,'fsdp'=8] {'seq'}, dimensions={2} | all-to-all | bytes 1769472 | tf_op jit(solution)/shard_map/all_to_all | solution.py:281
  442.6 27.9 %while.27 = (s32[]{:T(128)}, bf16[3,512,288]{1,2,0:T(8,128)(2,1)}, bf16[3,512,288]{1,2,0:T(8,128)(2,1)}, bf16[3,512,288]{1,2,0:T(8,128)(2,1)}, bf16[3,512,288]{1...) while((s32[]{:T(128)}, bf16[3,512,288]{1,2,0:T(8,128)(2,1)}, ...), condition=%wide.region_12.13_spmd, body=%wide.region_10.12_spmd.sunk | while | flops 767539200 | bytes 27184272 | solution.py:288
  470.5 3.4 copy.81
  473.9 3.6 all-to-all-start.7
  478.0 18.1 %all-to-all-done.7 = bf16[3,512,288]{2,0,1:T(4,128)(2,1)S(1)} async-done(((bf16[3,512,288]{2,0,1:T(4,128)(2,1)}), bf16[3,512,288]{2,0,1:T(4,128)(2,1)S(1)}, u32[]{:S(2)}, u32[]{:S(2)}) %all-to-all-start.7) | async-done | bytes 884768 | tf_op jit(solution)/shard_map/all_to_all | solution.py:294
  496.1 2.8 convert_reduce_fusion
  501.0 4.0 fusion.54
  505.1 2.8 copy.77
  507.9 21.9 %all_to_all.133 = bf16[3,512,288]{2,0,1:T(4,128)(2,1)S(1)} all-to-all(bf16[3,512,288]{2,0,1:T(4,128)(2,1)S(1)} %copy.77), channel_id=1, replica_groups=mesh['seq'=4,'fsdp'=8] {'seq'}, dimensions={1} | all-to-all | bytes 1769472 | tf_op jit(solution)/shard_map/all_to_all | solution.py:292
  533.3 5.2 fusion.52
  538.6 2.8 copy.79
  541.4 20.5 %all_to_all.134 = bf16[3,512,288]{2,0,1:T(4,128)(2,1)S(1)} all-to-all(bf16[3,512,288]{2,0,1:T(4,128)(2,1)S(1)} %copy.79), channel_id=1, replica_groups=mesh['seq'=4,'fsdp'=8] {'seq'}, dimensions={1} | all-to-all | bytes 1769472 | tf_op jit(solution)/shard_map/all_to_all | solution.py:293
  564.7 5.2 fusion.53
  571.4 11.5 fusion.33
  584.1 15.7 %fusion.43 = f32[4304,1152]{1,0:T(8,128)} fusion(bf16[384,1152]{1,0:T(8,128)(2,1)S(1)} %bitcast.214, f32[384,4304]{0,1:T(8,128)} %get-tuple-element.275), kind=kOutput, calls=%fused_computation.126 | convolution fusion | flops 3822778368 | bytes 27328512 | tf_op jit(solution)/shard_map/dot_general | solution.py:16
  599.8 387.6 %fusion = f32[544,1152]{1,0:T(8,128)} fusion(f32[4304,1152]{1,0:T(8,128)} %fusion.43), kind=kCustom, calls=%all-reduce-scatter | all-reduce-scatter fusion | flops 5013505 | bytes 22340096
  991.7 9.9 concatenate.7
  1001.6 3.4 constant_dynamic-slice_fusion.8
  1005.0 45.8 %reduce-scatter.16.cloned.1.call-done = f32[144,4304]{1,0:T(8,128)} async-done(((f32[1152,4304]{1,0:T(8,128)}), f32[144,4304]{1,0:T(8,128)}) %reduce-scatter.16.cloned.1.call-update) | async-done | bytes 2479120 | tf_op jit(solution)/shard_map/reduce_scatter | solution.py:330
  1052.2 11.6 fusion.29
  1066.0 3.4 fusion.51
  1071.8 2.9 multiply_reduce_fusion.1
  1074.8 29.1 %all-reduce.20 = (f32[1152]{0:T(1024)S(1)}, f32[1152]{0:T(1024)S(1)}, f32[1152]{0:T(1024)S(1)}, f32[1152]{0:T(1024)S(1)}, f32[1152]{0:T(1024)S(1)}, /*index=5*/f...) all-reduce(f32[1152]{0:T(1024)S(1)} %get-tuple-element.175, ...), channel_id=2, replica_groups=mesh['seq'=4,'fsdp'=8] {'fsdp'}, use_global_device_ids=true, to_apply=%region_16.17.clone | all-reduce | flops 13520 | bytes 108160
  1104.6 17.3 %all-reduce.21 = (f32[144]{0:T(256)}, f32[144]{0:T(256)}, f32[144]{0:T(256)}, f32[144]{0:T(256)}, f32[144]{0:T(256)}, /*index=5*/f32[144]{0:T(256)}, f32[144]{0:T(256)}, f32[538]{0:T(1024)}, f32[144]{0:T(256)}) all-reduce(f32[144]{0:T(256)S(1)} %dynamic-slice.10, ...), channel_id=1, replica_groups=mesh['seq'=4,'fsdp'=8] {'seq'}, use_global_device_ids=true, to_apply=%region_17.18 | all-reduce | flops 1690 | bytes 13520 | tf_op jit(solution)/shard_map/psum | solution.py:335
  1121.8 3.3 multiply_add_fusion
  1125.1 92.1 %all-reduce.26.cloned.1.call-done = (f32[144,1152]{1,0:T(8,128)}, f32[144,1152]{1,0:T(8,128)}, f32[144,1152]{1,0:T(8,128)}, f32[144,1152]{1,0:T(8,128)}, f32[144,4304]{1,0:T(8,128)}, /*index=5*/f32[538,1152]{1,0:T(8,128)}) async-done(((f32[144,1152]{1,0:T(8,128)}, f32[144,1152]{1,0:T(8,128)}, f32[144,1152]{1,0:T(8,128)}, f32[144,1152]{1,0:T(8,128)}, f32[144,4304]{1,0:T(8,128)}, ...) | async-done | bytes 7612432 | tf_op jit(solution)/shard_map/psum | solution.py:335
  (334 shorter events, 120.2 us)
Async XLA Ops:
  7.2 81.5 %copy-start.52 = (u32[32]{0:T(128)S(1)}, u32[32]{0:T(128)}, u32[]{:S(2)}) copy-start(u32[32]{0:T(128)} %constant.144) | copy-start | bytes 388
  7.2 77.5 %copy-start = (bf16[3,128,1152]{2,1,0:T(8,128)(2,1)S(1)}, bf16[3,128,1152]{2,1,0:T(8,128)(2,1)}, u32[]{:S(2)}) copy-start(bf16[3,128,1152]{2,1,0:T(8,128)(2,1)} %param.22) | copy-start | bytes 2654212
  7.2 83.4 %copy-start.57 = (bf16[144]{0:T(256)(128)(2,1)S(1)}, bf16[144]{0:T(256)(128)(2,1)}, u32[]{:S(2)}) copy-start(bf16[144]{0:T(256)(128)(2,1)} %param.24) | copy-start | bytes 868
  7.2 83.7 %copy-start.58 = (bf16[144]{0:T(256)(128)(2,1)S(1)}, bf16[144]{0:T(256)(128)(2,1)}, u32[]{:S(2)}) copy-start(bf16[144]{0:T(256)(128)(2,1)} %param.30) | copy-start | bytes 868
  7.2 83.9 %copy-start.59 = (bf16[144]{0:T(256)(128)(2,1)S(1)}, bf16[144]{0:T(256)(128)(2,1)}, u32[]{:S(2)}) copy-start(bf16[144]{0:T(256)(128)(2,1)} %param.29) | copy-start | bytes 868
  7.2 84.1 %copy-start.60 = (bf16[144]{0:T(256)(128)(2,1)S(1)}, bf16[144]{0:T(256)(128)(2,1)}, u32[]{:S(2)}) copy-start(bf16[144]{0:T(256)(128)(2,1)} %param.32) | copy-start | bytes 868
  7.3 84.4 %copy-start.61 = (bf16[144]{0:T(256)(128)(2,1)S(1)}, bf16[144]{0:T(256)(128)(2,1)}, u32[]{:S(2)}) copy-start(bf16[144]{0:T(256)(128)(2,1)} %param.33) | copy-start | bytes 868
  7.3 84.6 %copy-start.62 = (bf16[144]{0:T(256)(128)(2,1)S(1)}, bf16[144]{0:T(256)(128)(2,1)}, u32[]{:S(2)}) copy-start(bf16[144]{0:T(256)(128)(2,1)} %param.34) | copy-start | bytes 868
  7.3 84.9 %copy-start.63 = (bf16[144]{0:T(256)(128)(2,1)S(1)}, bf16[144]{0:T(256)(128)(2,1)}, u32[]{:S(2)}) copy-start(bf16[144]{0:T(256)(128)(2,1)} %param.38) | copy-start | bytes 868
  7.3 85.1 %copy-start.64 = (bf16[144]{0:T(256)(128)(2,1)S(1)}, bf16[144]{0:T(256)(128)(2,1)}, u32[]{:S(2)}) copy-start(bf16[144]{0:T(256)(128)(2,1)} %param.25) | copy-start | bytes 868
  7.3 85.4 %copy-start.54 = (bf16[538]{0:T(1024)(128)(2,1)S(1)}, bf16[538]{0:T(1024)(128)(2,1)}, u32[]{:S(2)}) copy-start(bf16[538]{0:T(1024)(128)(2,1)} %param.36) | copy-start | bytes 3232
  7.3 172.6 %all-gather.10.cloned.1.call-start = ((), (), s32[]{:S(2)}) async-start(), calls=%async_computation.14 | async-start | bytes 2985984 | tf_op jit(solution)/shard_map/all_gather | solution.py:165
  8.0 183.9 %all-gather.12.cloned.1.call-start = ((), (), s32[]{:S(2)}) async-start(), calls=%async_computation.15 | async-start | bytes 2985984 | tf_op jit(solution)/shard_map/all_gather | solution.py:166
  8.8 190.5 %all-gather.8.cloned.1.call-start = ((), (), s32[]{:S(2)}) async-start(), calls=%async_computation.13 | async-start | bytes 2985984 | tf_op jit(solution)/shard_map/all_gather | solution.py:167
  9.5 305.8 %all-gather.14.cloned.1.call-start = ((), (), s32[]{:S(2)}) async-start(), calls=%async_computation.16 | async-start | bytes 2985984 | tf_op jit(solution)/shard_map/all_gather | solution.py:170
  10.1 310.8 %all-gather.18.cloned.1.call-start = ((), (), s32[]{:S(2)}) async-start(), calls=%async_computation.23 | async-start | bytes 11280384 | tf_op jit(solution)/shard_map/all_gather | solution.py:176
  10.7 163.8 %copy-start.49 = (s32[3,512]{1,0:T(4,128)S(1)}, s32[3,512]{1,0:T(4,128)}, u32[]{:S(2)}) copy-start(s32[3,512]{1,0:T(4,128)} %param.23) | copy-start | bytes 18436
  10.7 382.1 %all-gather.16.cloned.1.call-start = ((), (), s32[]{:S(2)}) async-start(), calls=%async_computation.17 | async-start | bytes 11280384 | tf_op jit(solution)/shard_map/all_gather | solution.py:241
  10.7 30.6 %collective-permute-start = (bf16[144,4304]{1,0:T(8,128)(2,1)}, bf16[144,4304]{1,0:T(8,128)(2,1)S(1)}, u32[]{:S(2)}, u32[]{:S(2)}) collective-permute-start(bf16[144,4304]{1,0:T(8,128)(2,1)} %param.35), channel_id=1, source_target_pairs={{0,1},{1,2},{2,3},{3,4},{4,5},{5,6},{6,7},{7,0},{8,9},{9,10},{10,1... | collective-permute-start | bytes 3718664 | tf_op jit(solution)/shard_map/ppermute | solution.py:152
  41.4 43.5 %copy-start.14 = (bf16[144,4304]{1,0:T(8,128)(2,1)}, bf16[144,4304]{1,0:T(8,128)(2,1)S(1)}, u32[]{:S(2)}) copy-start(bf16[144,4304]{1,0:T(8,128)(2,1)S(1)} %collective-permute-done) | copy-start | bytes 3718660
  41.4 30.4 %collective-permute-start.1 = (bf16[144,4304]{1,0:T(8,128)(2,1)S(1)}, bf16[144,4304]{1,0:T(8,128)(2,1)}, u32[]{:S(2)}, u32[]{:S(2)}) collective-permute-start(bf16[144,4304]{1,0:T(8,128)(2,1)S(1)} %collective-permute-done), channel_id=1, source_target_pairs={{0,1},{1,2},{2,3},{3,4},{4,5},{5,6},{6,7},{7,0},{8,9},{9,10},{10,1... | collective-permute-start | bytes 3718664 | tf_op jit(solution)/shard_map/ppermute | solution.py:152
  43.0 42.1 %collective-permute-start.4 = (bf16[144,4304]{1,0:T(8,128)(2,1)}, bf16[144,4304]{1,0:T(8,128)(2,1)S(1)}, u32[]{:S(2)}, u32[]{:S(2)}) collective-permute-start(bf16[144,4304]{1,0:T(8,128)(2,1)} %param.35), channel_id=1, source_target_pairs={{0,7},{1,0},{2,1},{3,2},{4,3},{5,4},{6,5},{7,6},{8,15},{9,8},{10,9... | collective-permute-start | bytes 3718664 | tf_op jit(solution)/shard_map/ppermute | solution.py:155
  71.8 102.6 %collective-permute-start.2 = (bf16[144,4304]{1,0:T(8,128)(2,1)}, bf16[144,4304]{1,0:T(8,128)(2,1)}, u32[]{:S(2)}, u32[]{:S(2)}) collective-permute-start(bf16[144,4304]{1,0:T(8,128)(2,1)} %collective-permute-done.1), channel_id=1, source_target_pairs={{0,1},{1,2},{2,3},{3,4},{4,5},{5,6},{6,7},{7,0},{8,9},{9,10},{10,1... | collective-permute-start | bytes 3718664 | tf_op jit(solution)/shard_map/ppermute | solution.py:152
  85.0 99.3 %copy-start.11 = (bf16[144,4304]{1,0:T(8,128)(2,1)}, bf16[144,4304]{1,0:T(8,128)(2,1)S(1)}, u32[]{:S(2)}) copy-start(bf16[144,4304]{1,0:T(8,128)(2,1)S(1)} %collective-permute-done.4) | copy-start | bytes 3718660
  85.0 91.3 %collective-permute-start.5 = (bf16[144,4304]{1,0:T(8,128)(2,1)S(1)}, bf16[144,4304]{1,0:T(8,128)(2,1)S(1)}, u32[]{:S(2)}, u32[]{:S(2)}) collective-permute-start(bf16[144,4304]{1,0:T(8,128)(2,1)S(1)} %collective-permute-done.4), channel_id=1, source_target_pairs={{0,7},{1,0},{2,1},{3,2},{4,3},{5,4},{6,5},{7,6},{8,15},{9,8},{10,9... | collective-permute-start | bytes 3718664 | tf_op jit(solution)/shard_map/ppermute | solution.py:155
  88.7 95.6 %copy-start.42 = (f32[384]{0:T(512)}, f32[384]{0:T(512)S(1)}, u32[]{:S(2)}) copy-start(f32[384]{0:T(512)S(1)} %get-tuple-element.268) | copy-start | bytes 4612
  88.7 95.6 %copy-start.46 = (f32[3,128]{1,0:T(4,128)}, f32[3,128]{1,0:T(4,128)S(1)}, u32[]{:S(2)}) copy-start(f32[3,128]{1,0:T(4,128)S(1)} %get-tuple-element.269) | copy-start | bytes 4612
  173.2 11.2 copy-start.44
  174.5 44.0 %collective-permute-start.3 = (bf16[144,4304]{1,0:T(8,128)(2,1)}, bf16[144,4304]{1,0:T(8,128)(2,1)}, u32[]{:S(2)}, u32[]{:S(2)}) collective-permute-start(bf16[144,4304]{1,0:T(8,128)(2,1)} %collective-permute-done.2), channel_id=1, source_target_pairs={{0,1},{1,2},{2,3},{3,4},{4,5},{5,6},{6,7},{7,0},{8,9},{9,10},{10,1... | collective-permute-start | bytes 3718664 | tf_op jit(solution)/shard_map/ppermute | solution.py:152
  176.4 53.2 %copy-start.10 = (bf16[144,4304]{1,0:T(8,128)(2,1)}, bf16[144,4304]{1,0:T(8,128)(2,1)S(1)}, u32[]{:S(2)}) copy-start(bf16[144,4304]{1,0:T(8,128)(2,1)S(1)} %collective-permute-done.5) | copy-start | bytes 3718660
  176.4 54.4 %collective-permute-start.6 = (bf16[144,4304]{1,0:T(8,128)(2,1)S(1)}, bf16[144,4304]{1,0:T(8,128)(2,1)}, u32[]{:S(2)}, u32[]{:S(2)}) collective-permute-start(bf16[144,4304]{1,0:T(8,128)(2,1)S(1)} %collective-permute-done.5), channel_id=1, source_target_pairs={{0,7},{1,0},{2,1},{3,2},{4,3},{5,4},{6,5},{7,6},{8,15},{9,8},{10,9... | collective-permute-start | bytes 3718664 | tf_op jit(solution)/shard_map/ppermute | solution.py:155
  184.3 7.6 copy-start.25
  187.6 50.5 %all-to-all-start.1 = ((bf16[3,128,1152]{1,0,2:T(4,128)(2,1)}), bf16[3,128,1152]{1,0,2:T(4,128)(2,1)}, u32[]{:S(2)}, u32[]{:S(2)}) async-start(bf16[3,128,1152]{1,0,2:T(4,128)(2,1)} %copy.66), calls=%async_computation.1 | async-start | bytes 2359296 | tf_op jit(solution)/shard_map/all_to_all | solution.py:207
  221.0 5.2 copy-start.15
  238.2 6.8 copy-start.16
  238.2 19.3 %all-to-all-start = ((bf16[3,128,1152]{1,0,2:T(4,128)(2,1)}), bf16[3,128,1152]{1,0,2:T(4,128)(2,1)}, u32[]{:S(2)}, u32[]{:S(2)}) async-start(bf16[3,128,1152]{1,0,2:T(4,128)(2,1)} %copy.63), calls=%async_computation | async-start | bytes 2359296 | tf_op jit(solution)/shard_map/all_to_all | solution.py:213
  246.1 17.2 %copy-start.13 = (bf16[144,4304]{1,0:T(8,128)(2,1)S(1)}, bf16[144,4304]{1,0:T(8,128)(2,1)}, u32[]{:S(2)}) copy-start(bf16[144,4304]{1,0:T(8,128)(2,1)} %copy-done.11) | copy-start | bytes 3718660
  257.5 14.9 %all-to-all-start.2 = ((bf16[3,128,1152]{1,0,2:T(4,128)(2,1)}), bf16[3,128,1152]{1,0,2:T(4,128)(2,1)}, u32[]{:S(2)}, u32[]{:S(2)}) async-start(bf16[3,128,1152]{1,0,2:T(4,128)(2,1)} %copy.69), calls=%async_computation.2 | async-start | bytes 2359296 | tf_op jit(solution)/shard_map/all_to_all | solution.py:210
  292.3 16.7 %all-to-all-start.3 = ((bf16[3,512,288]{2,0,1:T(4,128)(2,1)}), bf16[3,512,288]{2,0,1:T(4,128)(2,1)}, u32[]{:S(2)}, u32[]{:S(2)}) async-start(bf16[3,512,288]{2,0,1:T(4,128)(2,1)} %copy.72), calls=%async_computation.3 | async-start | bytes 3145728 | tf_op jit(solution)/shard_map/all_to_all | solution.py:219
  296.6 708.3 %reduce-scatter.14.cloned.1.call-start = ((), (), s32[]{:S(2)}) async-start(), calls=%async_computation.21 | async-start | bytes 5971968 | tf_op jit(solution)/shard_map/reduce_scatter | solution.py:326
  332.8 9.1 copy-start.2
  332.8 9.1 copy-start.31
  332.8 9.1 copy-start.35
  332.8 9.1 copy-start.40
  392.8 11.1 copy-start.3
  392.8 11.1 copy-start.8
  392.8 11.1 copy-start.36
  470.5 7.0 copy-start.29
  470.5 7.0 copy-start.34
  470.5 7.0 copy-start.47
  470.5 7.0 copy-start.48
  473.9 22.2 %all-to-all-start.7 = ((bf16[3,512,288]{2,0,1:T(4,128)(2,1)}), bf16[3,512,288]{2,0,1:T(4,128)(2,1)S(1)}, u32[]{:S(2)}, u32[]{:S(2)}) async-start(bf16[3,512,288]{2,0,1:T(4,128)(2,1)} %copy.81), calls=%async_computation.7 | async-start | bytes 3145728 | tf_op jit(solution)/shard_map/all_to_all | solution.py:294
  477.5 527.5 %reduce-scatter.12.cloned.1.call-start = ((), (), s32[]{:S(2)}) async-start(), calls=%async_computation.20 | async-start | bytes 5971968 | tf_op jit(solution)/shard_map/reduce_scatter | solution.py:323
  501.0 4.0 copy-start.18
  505.1 499.9 %reduce-scatter.8.cloned.1.call-start = ((), (), s32[]{:S(2)}) async-start(), calls=%async_computation.18 | async-start | bytes 5971968 | tf_op jit(solution)/shard_map/reduce_scatter | solution.py:321
  538.5 466.5 %reduce-scatter.10.cloned.1.call-start = ((), (), s32[]{:S(2)}) async-start(), calls=%async_computation.19 | async-start | bytes 5971968 | tf_op jit(solution)/shard_map/reduce_scatter | solution.py:322
  569.9 480.9 %reduce-scatter.16.cloned.1.call-start = ((), (), s32[]{:S(2)}) async-start(), calls=%async_computation.22 | async-start | bytes 22560768 | tf_op jit(solution)/shard_map/reduce_scatter | solution.py:330
  583.0 634.3 %all-reduce.26.cloned.1.call-start = ((), (), s32[]{:S(2)}) async-start(), calls=%async_computation.24 | async-start | bytes 15335424 | tf_op jit(solution)/shard_map/psum | solution.py:335
  989.0 2.7 collective-permute-start.7
  1052.2 13.8 %copy-start.20 = (bf16[384,1152]{1,0:T(8,128)(2,1)S(1)}, bf16[384,1152]{1,0:T(8,128)(2,1)}, u32[]{:S(2)}) copy-start(bf16[384,1152]{1,0:T(8,128)(2,1)} %reshape.284) | copy-start | bytes 2654212
  1071.8 50.0 %copy-start.6 = (f32[384,1152]{1,0:T(8,128)S(1)}, f32[384,1152]{1,0:T(8,128)}, u32[]{:S(2)}) copy-start(f32[384,1152]{1,0:T(8,128)} %copy-done.5) | copy-start | bytes 5308420
  1217.2 4.1 copy-start.27
  1217.2 4.9 copy-start.26
  1217.2 5.8 copy-start.24
  (26 other events, 56.9 us)
Sparse Core Ops, SparseCore 0:
  9.8 45.9 all-gather.9
  57.4 49.1 all-gather.11
  108.3 42.0 all-gather.7
  151.9 41.8 all-gather.13
  195.3 101.3 all-gather.17
  298.2 94.5 all-gather.15
  410.6 58.8 reduce-scatter.13
  505.2 57.8 reduce-scatter.11
  565.4 74.5 reduce-scatter.7
  642.1 111.4 reduce-scatter.9
  756.0 294.6 reduce-scatter.15
  1055.6 161.5 all-reduce.25
